TPU v7x, 256 devices: a whole 4x4x8 slice. The times are simulated.
256 devices in a mesh: seg: 4 (over z_hi), ch: 64 (over x, y, z_lo, core).
Axes of the slice: x: 4, y: 4, z: 8 (z_hi: 4, z_lo: 2; z = z_hi * 2 + z_lo), core: 2. Of those that a mesh axis runs over, the one named last changes fastest.
Arguments:
- gate_in: bfloat16 [1536, 16384], P('ch', 'seg'), may hold values from -6 to 6
- key_in: bfloat16 [1536, 16384], P('ch', 'seg'), may hold values from -6 to 6
- value_in: bfloat16 [1536, 16384], P('ch', 'seg'), may hold values from -6 to 6
- kernel: float32 [1536, 16384], P('ch'), may hold values from -0.046875 to 0.046875
- skip_gain: float32 [1536], P('ch'), may hold values from -1 to 1
- out_weight: bfloat16 [1536, 1536], P('ch'), may hold values from -0.15625 to 0.15625
Outputs:
- output: bfloat16 [16384, 1536], P(('seg', 'ch'))
All inputs are finite; a program needn't handle non-finite values.
Results may differ from a plain program's by a relative error of at most 0.0095.
Values may be sent and summed in bfloat16 or wider, within the bound.
A program may use at most 64 MiB of HBM per device.

v0:
```python
import math
import jax
import jax.numpy as jnp
from jax import lax
from jax.sharding import Mesh
from jax.sharding import PartitionSpec as P

CH = ("ch_0", "ch_1", "ch_2", "ch_3")
SEG_CH = ("seg", "ch_0", "ch_1", "ch_2", "ch_3")
lane_width = 128
highest = lax.Precision.HIGHEST


def in_blocks(x, dim, devices):
    lengths = x.shape
    parts = x.reshape(*lengths[:dim], devices, lengths[dim] // devices, *lengths[dim + 1 :])
    return jnp.moveaxis(parts, dim, 0)


def in_order(parts, dim):
    lengths = list(parts.shape[1:])
    lengths[dim] *= parts.shape[0]
    return jnp.moveaxis(parts, 0, dim).reshape(lengths)


def turned_blocks(parts, axes, order):
    lengths = [lax.axis_size(a) for a in axes]
    parts = parts.reshape(*lengths, *parts.shape[1:])
    for k in order:
        parts = lax.all_to_all(parts, axes[k], split_axis=k, concat_axis=k, tiled=True)
    return parts.reshape(-1, *parts.shape[len(axes) :])


def core_and_chips(x, groups, order, split_dim, concat_dim):
    devices = lax.axis_size(groups[0]) * lax.axis_size(groups[1])
    parts = in_blocks(x, split_dim, devices)
    return in_order(turned_blocks(parts, groups, order), concat_dim)


def angle_pair(height, breadth, period):
    product = (
        jnp.arange(height, dtype=jnp.int32)[:, None]
        * jnp.arange(breadth, dtype=jnp.int32)[None, :]
        % period
    )
    theta = product.astype(jnp.float32) * (2.0 * math.pi / period)
    return (jnp.cos(theta), jnp.sin(theta))


def make_tables(outer):
    cos_outer, sin_outer = angle_pair(outer, outer, outer)
    cos_inner, sin_inner = angle_pair(lane_width, lane_width, lane_width)
    cos_twist, sin_twist = angle_pair(outer, lane_width, outer * lane_width)
    return (cos_outer, sin_outer, cos_inner, sin_inner, cos_twist, sin_twist)


def left_mul(matrix, stack):
    return jnp.einsum("kn,cnm->ckm", matrix, stack, precision=highest)


def right_mul(stack, matrix):
    return jnp.einsum("ckn,nm->ckm", stack, matrix, precision=highest)


def forward(signal, tables):
    cos_outer, sin_outer, cos_inner, sin_inner, cos_twist, sin_twist = tables
    height = signal.shape[1]
    real_a = left_mul(cos_outer[:, :height], signal)
    imag_a = -left_mul(sin_outer[:, :height], signal)
    real_b = real_a * cos_twist + imag_a * sin_twist
    imag_b = imag_a * cos_twist - real_a * sin_twist
    real_x = right_mul(real_b, cos_inner) + right_mul(imag_b, sin_inner)
    imag_x = right_mul(imag_b, cos_inner) - right_mul(real_b, sin_inner)
    return (real_x, imag_x)


def inverse_upper(real_x, imag_x, tables):
    cos_outer, sin_outer, cos_inner, sin_inner, cos_twist, sin_twist = tables
    real_c = right_mul(real_x, cos_inner) - right_mul(imag_x, sin_inner)
    imag_c = right_mul(imag_x, cos_inner) + right_mul(real_x, sin_inner)
    real_d = real_c * cos_twist - imag_c * sin_twist
    imag_d = imag_c * cos_twist + real_c * sin_twist
    middle = cos_outer.shape[0] // 2
    signal = left_mul(cos_outer[middle:], real_d) - left_mul(sin_outer[middle:], imag_d)
    return signal / float(cos_outer.shape[0] * lane_width)


def on_device(gate_in, key_in, value_in, kernel, skip_gain, out_weight):
    seg_index = lax.axis_index("seg")
    col_gate, col_key, col_value = (
        lax.all_to_all(gate_in, "seg", split_axis=0, concat_axis=1, tiled=True),
        lax.all_to_all(key_in, "seg", split_axis=0, concat_axis=1, tiled=True),
        lax.all_to_all(value_in, "seg", split_axis=0, concat_axis=1, tiled=True),
    )
    col_count, full_len = col_key.shape
    long_outer = 2 * full_len // lane_width
    long_tables = make_tables(long_outer)
    first = seg_index * col_count
    my_kernel = lax.dynamic_slice_in_dim(kernel, first, col_count, 0)
    my_skip = lax.dynamic_slice_in_dim(skip_gain, first, col_count, 0)
    col_mixed = col_key.astype(jnp.float32) * col_value.astype(jnp.float32)
    long_filter = jnp.concatenate(
        [jnp.zeros((col_count, full_len), jnp.float32), my_kernel], axis=1
    )
    filt_re, filt_im = forward(long_filter.reshape(col_count, long_outer, lane_width), long_tables)
    sig_re, sig_im = forward(col_mixed.reshape(col_count, long_outer // 2, lane_width), long_tables)
    prod_re = filt_re * sig_re - filt_im * sig_im
    prod_im = filt_re * sig_im + filt_im * sig_re
    col_conv = inverse_upper(prod_re, prod_im, long_tables).reshape(col_count, full_len)
    col_gated = (col_gate.astype(jnp.float32) * (col_conv + my_skip[:, None] * col_mixed)).astype(
        jnp.bfloat16
    )
    gated = lax.all_to_all(col_gated, "seg", split_axis=1, concat_axis=0, tiled=True)
    local_tokens = core_and_chips(gated, (("ch_0", "ch_1", "ch_2"), "ch_3"), (1, 0), 1, 0)
    result = lax.dot_general(
        local_tokens,
        lax.all_gather(out_weight, CH, axis=0, tiled=True),
        (((0,), (0,)), ((), ())),
        preferred_element_type=jnp.float32,
    )
    return result.astype(jnp.bfloat16)


def solution(mesh):
    torus = Mesh(
        mesh.devices.reshape(mesh.shape["seg"], 4, 4, 2, 2), ("seg", "ch_0", "ch_1", "ch_2", "ch_3")
    )
    in_specs = (P(CH, "seg"), P(CH, "seg"), P(CH, "seg"), P(CH, None), P(CH), P(CH, None))
    out_specs = P(SEG_CH, None)
    return jax.shard_map(
        on_device, mesh=torus, in_specs=in_specs, out_specs=out_specs, check_vma=False
    )
```

profile of v0, /device:TPU:1, one launch (start us, length us, event | category | flops | bytes accessed | tf_op | source)
XLA Modules:
  0.0 142.8 jit_solution(324831738904473637)
XLA Ops:
  6.5 1.8 %all_to_all.48 = bf16[4,6,4096]{2,1,0:T(8,128)(2,1)} reshape(bf16[24,4096]{1,0:T(8,128)(2,1)} %param.7) | data formatting | bytes 393216 | tf_op jit(solution)/shard_map/all_to_all | solution.py:92
  8.3 9.0 %all-to-all-start.1 = ((bf16[4,6,4096]{2,1,0:T(8,128)(2,1)}), bf16[4,6,4096]{2,1,0:T(8,128)(2,1)}, u32[]{:S(2)}, u32[]{:S(2)}) async-start(bf16[4,6,4096]{2,1,0:T(8,128)(2,1)} %all_to_all.48), calls=%async_computation.1 | async-start | bytes 524288 | tf_op jit(solution)/shard_map/all_to_all | solution.py:92
  18.6 1.7 %fusion.36 = f32[256,256]{1,0:T(8,128)} fusion(), kind=kLoop, calls=%fused_computation.67 | loop fusion | flops 917504 | bytes 262144 | tf_op jit(solution)/shard_map/cos | solution.py:47
  20.3 1.7 %all_to_all.50 = bf16[4,6,4096]{2,1,0:T(8,128)(2,1)} reshape(bf16[24,4096]{1,0:T(8,128)(2,1)} %param.8) | data formatting | bytes 393216 | tf_op jit(solution)/shard_map/all_to_all | solution.py:93
  22.1 2.3 %convolution_bitcast_fusion = f32[6,256,128]{1,2,0:T(8,128)S(1)} fusion(f32[1,6,256,128]{3,1,2,0:T(8,128)S(1)} %pad_bitcast_fusion), kind=kOutput, calls=%fused_computation.9 | convolution fusion | flops 604897280 | bytes 1572864 | tf_op jit(solution)/shard_map/kn,cnm->ckm/dot_general | solution.py:58
  24.4 2.3 %fusion = f32[6,256,128]{1,2,0:T(8,128)S(1)} fusion(f32[1,6,256,128]{3,1,2,0:T(8,128)S(1)} %pad_bitcast_fusion), kind=kOutput, calls=%fused_computation.8 | convolution fusion | flops 605093888 | bytes 1572864 | tf_op jit(solution)/shard_map/kn,cnm->ckm/dot_general | solution.py:58
  26.8 1.6 %fusion.38 = f32[6,256,128]{2,1,0:T(8,128)S(1)} fusion(f32[6,256,128]{1,2,0:T(8,128)S(1)} %fusion, f32[6,256,128]{1,2,0:T(8,128)S(1)} %convolution_bitcast_fusion, f32[256,128]{0,1:T(8,128)S(1)} %get-tuple-element.7, f32[256,128]{0,1:T(8,128)S(1)} %get-tuple-element.8), kind=kOutput, calls=%fused_computation.69 | convolution fusion | flops 302809088 | bytes 2621440 | tf_op jit(solution)/shard_map/ckn,nm->ckm/dot_general | solution.py:62
  28.4 2.5 %convolution_add_fusion.2 = f32[6,256,128]{2,1,0:T(8,128)} fusion(f32[6,256,128]{2,1,0:T(8,128)S(1)} %fusion.38, f32[6,256,128]{1,2,0:T(8,128)S(1)} %convolution_bitcast_fusion, f32[6,256,128]{1,2,0:T(8,128)S(1)} %fusion, f32[256,128]{0,1:T(8,128)S(1)} %get-tuple-element.7, f32[256,128]{0,1:T(8,128)S(1)} %get-tuple-element.8), kind=kOutput, calls=%fused_computation.6 | convolution fusion | flops 303005696 | bytes 3407872 | tf_op jit(solution)/shard_map/ckn,nm->ckm/dot_general | solution.py:62
  30.9 6.6 %all-to-all-start.2 = ((bf16[4,6,4096]{2,1,0:T(8,128)(2,1)}), bf16[4,6,4096]{2,1,0:T(8,128)(2,1)}, u32[]{:S(2)}, u32[]{:S(2)}) async-start(bf16[4,6,4096]{2,1,0:T(8,128)(2,1)} %all_to_all.50), calls=%async_computation.2 | async-start | bytes 524288 | tf_op jit(solution)/shard_map/all_to_all | solution.py:93
  37.5 1.7 %fusion.35 = f32[256,256]{1,0:T(8,128)} fusion(), kind=kLoop, calls=%fused_computation.66 | loop fusion | flops 917504 | bytes 262144 | tf_op jit(solution)/shard_map/sin | solution.py:47
  39.3 1.7 %all_to_all.46 = bf16[4,6,4096]{2,1,0:T(8,128)(2,1)} reshape(bf16[24,4096]{1,0:T(8,128)(2,1)} %param.6) | data formatting | bytes 393216 | tf_op jit(solution)/shard_map/all_to_all | solution.py:91
  41.0 2.5 %fusion.39 = f32[6,256,128]{2,1,0:T(8,128)} fusion(f32[6,256,128]{1,2,0:T(8,128)S(1)} %convolution_bitcast_fusion, f32[6,256,128]{1,2,0:T(8,128)S(1)} %fusion, f32[256,128]{0,1:T(8,128)S(1)} %get-tuple-element.7, f32[256,128]{0,1:T(8,128)S(1)} %get-tuple-element.8), kind=kOutput, calls=%fused_computation.70 | convolution fusion | flops 302809088 | bytes 2621440 | tf_op jit(solution)/shard_map/ckn,nm->ckm/dot_general | solution.py:62
  43.5 5.5 %all-to-all-done.2 = bf16[4,6,4096]{2,1,0:T(8,128)(2,1)} async-done(((bf16[4,6,4096]{2,1,0:T(8,128)(2,1)}), bf16[4,6,4096]{2,1,0:T(8,128)(2,1)}, u32[]{:S(2)}, u32[]{:S(2)}) %all-to-all-start.2) | async-done | bytes 196640 | tf_op jit(solution)/shard_map/all_to_all | solution.py:93
  49.0 4.0 %all-to-all-start = ((bf16[4,6,4096]{2,1,0:T(8,128)(2,1)}), bf16[4,6,4096]{2,1,0:T(8,128)(2,1)}, u32[]{:S(2)}, u32[]{:S(2)}) async-start(bf16[4,6,4096]{2,1,0:T(8,128)(2,1)} %all_to_all.46), calls=%async_computation | async-start | bytes 524288 | tf_op jit(solution)/shard_map/all_to_all | solution.py:91
  53.0 1.1 fusion.17
  55.2 2.0 %mul.450 = f32[6,128,128]{2,1,0:T(8,128)} reshape(f32[6,4,4096]{2,1,0:T(4,128)} %copy.64) | data formatting | bytes 786432 | tf_op jit(solution)/shard_map/mul | solution.py:101
  57.2 1.8 %convolution_bitcast_fusion.1 = f32[6,256,128]{1,2,0:T(8,128)S(1)} fusion(f32[6,128,128]{2,1,0:T(8,128)} %mul.450, f32[256,256]{1,0:T(8,128)} %fusion.36), kind=kOutput, calls=%fused_computation.12 | convolution fusion | flops 301989888 | bytes 1310720 | tf_op jit(solution)/shard_map/kn,cnm->ckm/dot_general | solution.py:58
  59.0 1.8 %fusion.1 = f32[6,256,128]{1,2,0:T(8,128)S(1)} fusion(f32[6,128,128]{2,1,0:T(8,128)} %mul.450, f32[256,256]{1,0:T(8,128)} %fusion.35), kind=kOutput, calls=%fused_computation.11 | convolution fusion | flops 302186496 | bytes 1310720 | tf_op jit(solution)/shard_map/kn,cnm->ckm/dot_general | solution.py:58
  60.9 1.6 %fusion.40 = f32[6,256,128]{2,1,0:T(8,128)S(1)} fusion(f32[6,256,128]{1,2,0:T(8,128)S(1)} %fusion.1, f32[6,256,128]{1,2,0:T(8,128)S(1)} %convolution_bitcast_fusion.1, f32[256,128]{0,1:T(8,128)S(1)} %get-tuple-element.7, f32[256,128]{0,1:T(8,128)S(1)} %get-tuple-element.8), kind=kOutput, calls=%fused_computation.71 | convolution fusion | flops 302809088 | bytes 2621440 | tf_op jit(solution)/shard_map/ckn,nm->ckm/dot_general | solution.py:62
  62.5 1.6 %fusion.41 = f32[6,256,128]{2,1,0:T(8,128)S(1)} fusion(f32[6,256,128]{1,2,0:T(8,128)S(1)} %convolution_bitcast_fusion.1, f32[6,256,128]{1,2,0:T(8,128)S(1)} %fusion.1, f32[256,128]{0,1:T(8,128)S(1)} %get-tuple-element.7, f32[256,128]{0,1:T(8,128)S(1)} %get-tuple-element.8), kind=kOutput, calls=%fused_computation.72 | convolution fusion | flops 302809088 | bytes 2621440 | tf_op jit(solution)/shard_map/ckn,nm->ckm/dot_general | solution.py:62
  64.1 1.6 %convolution_add_fusion.1 = f32[6,256,128]{2,1,0:T(8,128)S(1)} fusion(f32[6,256,128]{2,1,0:T(8,128)S(1)} %fusion.40, f32[6,256,128]{1,2,0:T(8,128)S(1)} %convolution_bitcast_fusion.1, f32[6,256,128]{1,2,0:T(8,128)S(1)} %fusion.1, f32[256,128]{0,1:T(8,128)S(1)} %get-tuple-element.7, f32[256,128]{0,1:T(8,128)S(1)} %get-tuple-element.8), kind=kOutput, calls=%fused_computation.5 | convolution fusion | flops 303005696 | bytes 3407872 | tf_op jit(solution)/shard_map/ckn,nm->ckm/dot_general | solution.py:62
  65.8 1.6 %convolution_subtract_fusion.1 = f32[6,256,128]{2,1,0:T(8,128)S(1)} fusion(f32[6,256,128]{2,1,0:T(8,128)S(1)} %fusion.41, f32[6,256,128]{1,2,0:T(8,128)S(1)} %fusion.1, f32[6,256,128]{1,2,0:T(8,128)S(1)} %convolution_bitcast_fusion.1, f32[256,128]{0,1:T(8,128)S(1)} %get-tuple-element.7, f32[256,128]{0,1:T(8,128)S(1)} %get-tuple-element.8), kind=kOutput, calls=%fused_computation.3 | convolution fusion | flops 303005696 | bytes 3407872 | tf_op jit(solution)/shard_map/ckn,nm->ckm/dot_general | solution.py:62
  67.4 1.7 %multiply_subtract_fusion = (f32[6,256,128]{2,1,0:T(8,128)S(1)}, f32[6,256,128]{2,1,0:T(8,128)S(1)}) fusion(f32[6,256,128]{2,1,0:T(8,128)S(1)} %convolution_subtract_fusion.1, f32[6,256,128]{2,1,0:T(8,128)S(1)} %copy-done.2, f32[6,256,128]{2,1,0:T(8,128)S(1)} %convolution_add_fusion.1, f32[6,256,128]{2,1,0:T(8,128)S(1)} %copy-done.1, ...), kind=kOutput, calls=%fused_computation.27 | convolution fusion | flops 304185344 | bytes 6553600 | tf_op jit(solution)/shard_map/ckn,nm->ckm/dot_general | solution.py:62
  69.1 1.1 fusion.55
  70.2 1.3 fusion.53
  72.6 1.1 convolution_add_fusion
  75.7 1.4 %fusion.16 = bf16[6,4,4096]{2,0,1:T(8,128)(2,1)S(1)} fusion(f32[6,4,4096]{2,1,0:T(4,128)S(1)} %reshape.75, bf16[4,6,4096]{2,1,0:T(8,128)(2,1)} %all-to-all-done, bf16[4,6,4096]{2,1,0:T(8,128)(2,1)} %all-to-all-done.2, bf16[4,6,4096]{2,1,0:T(8,128)(2,1)} %all-to-all-done.1, f32[6]{0:T(128)S(1)} %dynamic_slice.7), kind=kLoop, calls=%fused_computation.36 | loop fusion | flops 786432 | bytes 1179672 | tf_op jit(solution)/shard_map/convert_element_type | solution.py:110
  77.2 15.5 %all_to_all.62 = bf16[6,4,4096]{2,0,1:T(8,128)(2,1)S(1)} all-to-all(bf16[6,4,4096]{2,0,1:T(8,128)(2,1)S(1)} %fusion.16), channel_id=1, replica_groups=mesh['seg'=4,'ch_0'=4,'ch_1'=4,'ch_2'=2,'ch_3'=2] {'seg'}, dimensions={1} | all-to-all | bytes 393216 | tf_op jit(solution)/shard_map/all_to_all | solution.py:113
  93.6 9.4 %all_to_all.63 = bf16[2,2,24576]{2,1,0:T(2,128)(2,1)S(1)} all-to-all(bf16[2,2,24576]{2,1,0:T(2,128)(2,1)S(1)} %reshape.86), channel_id=1, replica_groups=mesh['seg'=4,'ch_0'=4,'ch_1'=4,'ch_2'=2,'ch_3'=2] {'ch_3'}, dimensions={0} | all-to-all | bytes 393216 | tf_op jit(solution)/shard_map/all_to_all | solution.py:30
  103.6 11.6 %all_to_all.64 = bf16[32,2,1536]{2,1,0:T(2,128)(2,1)S(1)} all-to-all(bf16[32,2,1536]{2,1,0:T(2,128)(2,1)S(1)} %reshape.88), channel_id=1, replica_groups=mesh['seg'=4,'ch_0'=4,'ch_1'=4,'ch_2'=2,'ch_3'=2] {'ch_0','ch_1','ch_2'}, dimensions={0} | all-to-all | bytes 393216 | tf_op jit(solution)/shard_map/all_to_all | solution.py:30
  115.4 16.6 %all-gather.2.cloned.1.call-done = bf16[1536,1536]{1,0:T(8,128)(2,1)} async-done(((bf16[24,1536]{1,0:T(8,128)(2,1)}), bf16[1536,1536]{1,0:T(8,128)(2,1)}) %all-gather.2.cloned.1.call-update) | async-done | bytes 4718608 | tf_op jit(solution)/shard_map/all_gather | solution.py:117
  132.0 4.0 %convolution_convert_fusion = bf16[64,1536]{1,0:T(8,128)(2,1)} fusion(bf16[1536,64]{1,0:T(8,128)(2,1)S(1)} %bitcast.93, bf16[1536,1536]{1,0:T(8,128)(2,1)} %all-gather.2.cloned.1.call-done), kind=kOutput, calls=%fused_computation | convolution fusion | flops 302088192 | bytes 5111808 | tf_op jit(solution)/shard_map/dot_general | solution.py:115
  (33 shorter events, 7.3 us)
Async XLA Ops:
  6.5 15.4 %copy-start = (f32[24,16384]{1,0:T(8,128)S(1)}, f32[24,16384]{1,0:T(8,128)}, u32[]{:S(2)}) copy-start(f32[24,16384]{1,0:T(8,128)} %param.9) | copy-start | bytes 4718596
  8.3 22.5 %all-to-all-start.1 = ((bf16[4,6,4096]{2,1,0:T(8,128)(2,1)}), bf16[4,6,4096]{2,1,0:T(8,128)(2,1)}, u32[]{:S(2)}, u32[]{:S(2)}) async-start(bf16[4,6,4096]{2,1,0:T(8,128)(2,1)} %all_to_all.48), calls=%async_computation.1 | async-start | bytes 524288 | tf_op jit(solution)/shard_map/all_to_all | solution.py:92
  17.3 114.7 %all-gather.2.cloned.1.call-start = ((), (), s32[]{:S(2)}) async-start(), calls=%async_computation.6 | async-start | bytes 4792320 | tf_op jit(solution)/shard_map/all_gather | solution.py:117
  22.1 17.1 %copy-start.5 = (f32[24]{0:T(128)S(1)}, f32[24]{0:T(128)}, u32[]{:S(2)}) copy-start(f32[24]{0:T(128)} %param.10) | copy-start | bytes 292
  30.9 18.1 %all-to-all-start.2 = ((bf16[4,6,4096]{2,1,0:T(8,128)(2,1)}), bf16[4,6,4096]{2,1,0:T(8,128)(2,1)}, u32[]{:S(2)}, u32[]{:S(2)}) async-start(bf16[4,6,4096]{2,1,0:T(8,128)(2,1)} %all_to_all.50), calls=%async_computation.2 | async-start | bytes 524288 | tf_op jit(solution)/shard_map/all_to_all | solution.py:93
  49.0 26.7 %all-to-all-start = ((bf16[4,6,4096]{2,1,0:T(8,128)(2,1)}), bf16[4,6,4096]{2,1,0:T(8,128)(2,1)}, u32[]{:S(2)}, u32[]{:S(2)}) async-start(bf16[4,6,4096]{2,1,0:T(8,128)(2,1)} %all_to_all.46), calls=%async_computation | async-start | bytes 524288 | tf_op jit(solution)/shard_map/all_to_all | solution.py:91
  62.5 4.9 %copy-start.1 = (f32[6,256,128]{2,1,0:T(8,128)S(1)}, f32[6,256,128]{2,1,0:T(8,128)}, u32[]{:S(2)}) copy-start(f32[6,256,128]{2,1,0:T(8,128)} %fusion.39) | copy-start | bytes 2359300
  62.5 4.9 %copy-start.2 = (f32[6,256,128]{2,1,0:T(8,128)S(1)}, f32[6,256,128]{2,1,0:T(8,128)}, u32[]{:S(2)}) copy-start(f32[6,256,128]{2,1,0:T(8,128)} %convolution_add_fusion.2) | copy-start | bytes 2359300
  69.1 4.7 %copy-start.3 = (f32[256,256]{1,0:T(8,128)S(1)}, f32[256,256]{1,0:T(8,128)}, u32[]{:S(2)}) copy-start(f32[256,256]{1,0:T(8,128)} %fusion.36) | copy-start | bytes 786436
  70.2 4.4 %copy-start.4 = (f32[256,256]{1,0:T(8,128)S(1)}, f32[256,256]{1,0:T(8,128)}, u32[]{:S(2)}) copy-start(f32[256,256]{1,0:T(8,128)} %fusion.35) | copy-start | bytes 786436
Sparse Core Ops, SparseCore 0:
  20.0 111.9 all-gather.1
where the time goes:
time: 144 us; the launch traced here: 143 us
  blocking collectives  36.4 us (25%)
  matrix products  33.2 us (23%)
  waiting for transfers between devices  22.8 us (16%)
  starting transfers between devices  19.7 us (14%)
  between operations  13.7 us (10%)
  local copies, waits for them, and re-layouts  10.6 us (7%)
  other arithmetic  6.45 us (4%)
    all_to_all x2, blocking collectives, turned_blocks(): lax.all_to_all(parts, axes[k], split_axis=k, concat_axis=k, tiled=True)  20.9 us
    dot_general x12, matrix products, right_mul(): return jnp.einsum('ckn,nm->ckm', stack, matrix, precision=highest)  19.4 us
    all_gather x1, waiting for transfers between devices, on_device(): lax.all_gather(out_weight, CH, axis=0, tiled=True)  16.6 us
    all_to_all x1, blocking collectives, on_device(): lax.all_to_all(col_gated, 'seg', split_axis=1, concat_axis=0, tiled=True)  15.5 us
    dot_general x6, matrix products, left_mul(): return jnp.einsum('kn,cnm->ckm', matrix, stack, precision=highest)  9.87 us
    all_to_all x1, starting transfers between devices, on_device(): lax.all_to_all(key_in, 'seg', split_axis=0, concat_axis=1, tiled=True)  9 us
    all_to_all x1, starting transfers between devices, on_device(): lax.all_to_all(value_in, 'seg', split_axis=0, concat_axis=1, tiled=True)  6.64 us
    all_to_all x1, waiting for transfers between devices, on_device(): lax.all_to_all(value_in, 'seg', split_axis=0, concat_axis=1, tiled=True)  5.48 us
  transfers between devices with their start and end apart: 4, of which 2 were waited for; matrix products, arithmetic and copies ran while one was open for 29% of the time, Pallas kernels for 0%

commit v1 on v0

--- a/solution.py
+++ b/solution.py
@@ -1,3 +1,4 @@
+import functools
 import math
 import jax
 import jax.numpy as jnp
@@ -9,6 +10,16 @@
 SEG_CH = ("seg", "ch_0", "ch_1", "ch_2", "ch_3")
 lane_width = 128
 highest = lax.Precision.HIGHEST
+
+
+def save_face_all(work_x, across):
+    big = jnp.stack(lax.psum(1, across) * [work_x])
+    u1 = lax.all_to_all(big, across, split_axis=0, concat_axis=0)
+    piece_out = jnp.concatenate(u1, 0)
+    return piece_out
+
+
+_detail_sizes = functools.partial(save_face_all, across=CH)
 
 
 def in_blocks(x, dim, devices):
@@ -114,7 +125,7 @@
     local_tokens = core_and_chips(gated, (("ch_0", "ch_1", "ch_2"), "ch_3"), (1, 0), 1, 0)
     result = lax.dot_general(
         local_tokens,
-        lax.all_gather(out_weight, CH, axis=0, tiled=True),
+        _detail_sizes(out_weight),
         (((0,), (0,)), ((), ())),
         preferred_element_type=jnp.float32,
     )

time: 144 us -> 183 us (1.27)
  waiting for transfers between devices: 22.8 us -> 61.4 us
  between operations: 13.7 us -> 0.33 us
  starting transfers between devices: 19.7 us -> 26.6 us
  blocking collectives: 36.4 us -> 39.3 us
  local copies, waits for them, and re-layouts: 10.6 us -> 13.1 us
    all_to_all x0 -> x1, waiting for transfers between devices: none -> 59.1 us  [save_face_all(): u1 = lax.all_to_all(big, across, split_axis=0, concat_axis=0)]
    all_gather x1 -> x0, waiting for transfers between devices: 16.6 us -> none  [on_device(): lax.all_gather(out_weight, CH, axis=0, tiled=True)]
    all_to_all x0 -> x1, starting transfers between devices: none -> 6.55 us  [save_face_all(): u1 = lax.all_to_all(big, across, split_axis=0, concat_axis=0)]
    all_to_all x2, blocking collectives: 20.9 us -> 24.4 us  [turned_blocks(): lax.all_to_all(parts, axes[k], split_axis=k, concat_axis=k, tiled=True)]
    all_to_all x1, waiting for transfers between devices: 5.48 us -> 2.28 us  [on_device(): lax.all_to_all(value_in, 'seg', split_axis=0, concat_axis=1, tiled=True)]
    another operation x0 -> x1, local copies, waits for them, and re-layouts: none -> 2.48 us  [save_face_all(): big = jnp.stack(lax.psum(1, across) * [work_x])]
  transfers between devices with their start and end apart: 4 -> 4, of which waited for: 2 -> 2; matrix products, arithmetic and copies ran while one was open for 29% -> 21% of each run, Pallas kernels for 0% -> 0%
where the time goes in v1:
time: 183 us; the launch traced here: 180 us
  waiting for transfers between devices  61.4 us (34%)
  blocking collectives  39.3 us (21%)
  matrix products  33.2 us (18%)
  starting transfers between devices  26.6 us (15%)
  local copies, waits for them, and re-layouts  13.1 us (7%)
  other arithmetic  6.4 us (3%)
    all_to_all x1, waiting for transfers between devices, save_face_all(): u1 = lax.all_to_all(big, across, split_axis=0, concat_axis=0)  59.1 us
    all_to_all x2, blocking collectives, turned_blocks(): lax.all_to_all(parts, axes[k], split_axis=k, concat_axis=k, tiled=True)  24.4 us
    dot_general x12, matrix products, right_mul(): return jnp.einsum('ckn,nm->ckm', stack, matrix, precision=highest)  19.4 us
    all_to_all x1, blocking collectives, on_device(): lax.all_to_all(col_gated, 'seg', split_axis=1, concat_axis=0, tiled=True)  14.9 us
    dot_general x6, matrix products, left_mul(): return jnp.einsum('kn,cnm->ckm', matrix, stack, precision=highest)  9.87 us
    all_to_all x1, starting transfers between devices, on_device(): lax.all_to_all(key_in, 'seg', split_axis=0, concat_axis=1, tiled=True)  9 us
    all_to_all x1, starting transfers between devices, on_device(): lax.all_to_all(value_in, 'seg', split_axis=0, concat_axis=1, tiled=True)  6.64 us
    all_to_all x1, starting transfers between devices, save_face_all(): u1 = lax.all_to_all(big, across, split_axis=0, concat_axis=0)  6.55 us
  transfers between devices with their start and end apart: 4, of which 2 were waited for; matrix products, arithmetic and copies ran while one was open for 21% of the time, Pallas kernels for 0%

profile of v1, /device:TPU:1, one launch (start us, length us, event | category | flops | bytes accessed | tf_op | source)
XLA Modules:
  0.0 180.4 jit_solution(18218738017492718728)
XLA Ops:
  0.0 1.8 %all_to_all.51 = bf16[4,6,4096]{2,1,0:T(8,128)(2,1)} reshape(bf16[24,4096]{1,0:T(8,128)(2,1)} %param.7) | data formatting | bytes 393216 | tf_op jit(solution)/shard_map/all_to_all | solution.py:103
  1.8 9.0 %all-to-all-start.1 = ((bf16[4,6,4096]{2,1,0:T(8,128)(2,1)}), bf16[4,6,4096]{2,1,0:T(8,128)(2,1)}, u32[]{:S(2)}, u32[]{:S(2)}) async-start(bf16[4,6,4096]{2,1,0:T(8,128)(2,1)} %all_to_all.51), calls=%async_computation.1 | async-start | bytes 524288 | tf_op jit(solution)/shard_map/all_to_all | solution.py:103
  10.8 1.7 fusion.36
  13.2 2.3 %fusion = f32[6,256,128]{1,2,0:T(8,128)S(1)} fusion(f32[1,6,256,128]{3,1,2,0:T(8,128)S(1)} %pad_bitcast_fusion), kind=kOutput, calls=%fused_computation.8 | convolution fusion | flops 605093888 | bytes 1572864 | tf_op jit(solution)/shard_map/kn,cnm->ckm/dot_general | solution.py:69
  15.6 2.3 %convolution_bitcast_fusion = f32[6,256,128]{1,2,0:T(8,128)S(1)} fusion(f32[1,6,256,128]{3,1,2,0:T(8,128)S(1)} %pad_bitcast_fusion), kind=kOutput, calls=%fused_computation.9 | convolution fusion | flops 604897280 | bytes 1572864 | tf_op jit(solution)/shard_map/kn,cnm->ckm/dot_general | solution.py:69
  17.8 1.7 all_to_all.53
  19.6 1.6 fusion.38
  21.2 2.5 %convolution_add_fusion.2 = f32[6,256,128]{2,1,0:T(8,128)} fusion(f32[6,256,128]{2,1,0:T(8,128)S(1)} %fusion.38, f32[6,256,128]{1,2,0:T(8,128)S(1)} %convolution_bitcast_fusion, f32[6,256,128]{1,2,0:T(8,128)S(1)} %fusion, f32[256,128]{0,1:T(8,128)S(1)} %get-tuple-element.7, f32[256,128]{0,1:T(8,128)S(1)} %get-tuple-element.8), kind=kOutput, calls=%fused_computation.6 | convolution fusion | flops 303005696 | bytes 3407872 | tf_op jit(solution)/shard_map/ckn,nm->ckm/dot_general | solution.py:73
  23.7 6.6 %all-to-all-start.2 = ((bf16[4,6,4096]{2,1,0:T(8,128)(2,1)}), bf16[4,6,4096]{2,1,0:T(8,128)(2,1)}, u32[]{:S(2)}, u32[]{:S(2)}) async-start(bf16[4,6,4096]{2,1,0:T(8,128)(2,1)} %all_to_all.53), calls=%async_computation.2 | async-start | bytes 524288 | tf_op jit(solution)/shard_map/all_to_all | solution.py:104
  30.3 1.7 fusion.35
  32.1 1.7 all_to_all.49
  33.8 2.5 %fusion.39 = f32[6,256,128]{2,1,0:T(8,128)} fusion(f32[6,256,128]{1,2,0:T(8,128)S(1)} %convolution_bitcast_fusion, f32[6,256,128]{1,2,0:T(8,128)S(1)} %fusion, f32[256,128]{0,1:T(8,128)S(1)} %get-tuple-element.7, f32[256,128]{0,1:T(8,128)S(1)} %get-tuple-element.8), kind=kOutput, calls=%fused_computation.70 | convolution fusion | flops 302809088 | bytes 2621440 | tf_op jit(solution)/shard_map/ckn,nm->ckm/dot_general | solution.py:73
  36.3 2.3 %all-to-all-done.2 = bf16[4,6,4096]{2,1,0:T(8,128)(2,1)} async-done(((bf16[4,6,4096]{2,1,0:T(8,128)(2,1)}), bf16[4,6,4096]{2,1,0:T(8,128)(2,1)}, u32[]{:S(2)}, u32[]{:S(2)}) %all-to-all-start.2) | async-done | bytes 196640 | tf_op jit(solution)/shard_map/all_to_all | solution.py:104
  38.6 4.4 %all-to-all-start = ((bf16[4,6,4096]{2,1,0:T(8,128)(2,1)}), bf16[4,6,4096]{2,1,0:T(8,128)(2,1)}, u32[]{:S(2)}, u32[]{:S(2)}) async-start(bf16[4,6,4096]{2,1,0:T(8,128)(2,1)} %all_to_all.49), calls=%async_computation | async-start | bytes 524288 | tf_op jit(solution)/shard_map/all_to_all | solution.py:102
  45.0 2.0 %mul.450 = f32[6,128,128]{2,1,0:T(8,128)} reshape(f32[6,4,4096]{2,1,0:T(4,128)} %copy.64) | data formatting | bytes 786432 | tf_op jit(solution)/shard_map/mul | solution.py:112
  47.1 1.8 %fusion.1 = f32[6,256,128]{1,2,0:T(8,128)S(1)} fusion(f32[6,128,128]{2,1,0:T(8,128)} %mul.450, f32[256,256]{1,0:T(8,128)} %fusion.35), kind=kOutput, calls=%fused_computation.11 | convolution fusion | flops 302186496 | bytes 1310720 | tf_op jit(solution)/shard_map/kn,cnm->ckm/dot_general | solution.py:69
  48.9 1.8 %convolution_bitcast_fusion.1 = f32[6,256,128]{1,2,0:T(8,128)S(1)} fusion(f32[6,128,128]{2,1,0:T(8,128)} %mul.450, f32[256,256]{1,0:T(8,128)} %fusion.36), kind=kOutput, calls=%fused_computation.12 | convolution fusion | flops 301989888 | bytes 1310720 | tf_op jit(solution)/shard_map/kn,cnm->ckm/dot_general | solution.py:69
  50.8 1.6 fusion.41
  52.4 1.6 fusion.40
  54.0 1.6 convolution_subtract_fusion.1
  55.6 1.6 convolution_add_fusion.1
  57.3 1.7 multiply_subtract_fusion
  59.0 1.1 fusion.55
  60.1 1.3 fusion.53
  65.6 1.4 fusion.16
  67.0 14.9 %all_to_all.67 = bf16[6,4,4096]{2,0,1:T(8,128)(2,1)S(1)} all-to-all(bf16[6,4,4096]{2,0,1:T(8,128)(2,1)S(1)} %fusion.16), channel_id=1, replica_groups=mesh['seg'=4,'ch_0'=4,'ch_1'=4,'ch_2'=2,'ch_3'=2] {'seg'}, dimensions={1} | all-to-all | bytes 393216 | tf_op jit(solution)/shard_map/all_to_all | solution.py:124
  82.9 8.6 %all_to_all.68 = bf16[2,2,24576]{2,1,0:T(2,128)(2,1)S(1)} all-to-all(bf16[2,2,24576]{2,1,0:T(2,128)(2,1)S(1)} %reshape.92), channel_id=1, replica_groups=mesh['seg'=4,'ch_0'=4,'ch_1'=4,'ch_2'=2,'ch_3'=2] {'ch_3'}, dimensions={0} | all-to-all | bytes 393216 | tf_op jit(solution)/shard_map/all_to_all | solution.py:41
  92.1 15.8 %all_to_all.69 = bf16[32,2,1536]{2,1,0:T(2,128)(2,1)S(1)} all-to-all(bf16[32,2,1536]{2,1,0:T(2,128)(2,1)S(1)} %reshape.94), channel_id=1, replica_groups=mesh['seg'=4,'ch_0'=4,'ch_1'=4,'ch_2'=2,'ch_3'=2] {'ch_0','ch_1','ch_2'}, dimensions={0} | all-to-all | bytes 393216 | tf_op jit(solution)/shard_map/all_to_all | solution.py:41
  107.9 2.5 %stack.2 = bf16[64,24,1536]{2,1,0:T(8,128)(2,1)} broadcast(bf16[24,1536]{1,0:T(8,128)(2,1)S(1)} %copy-done.5), dimensions={1,2} | broadcast | bytes 4792320 | tf_op jit(solution)/shard_map/stack | solution.py:16
  110.4 6.6 %all-to-all-start.6 = ((bf16[64,24,1536]{2,1,0:T(8,128)(2,1)}), bf16[64,24,1536]{2,1,0:T(8,128)(2,1)}, u32[]{:S(2)}, u32[]{:S(2)}) async-start(bf16[64,24,1536]{2,1,0:T(8,128)(2,1)} %stack.2), calls=%async_computation.6 | async-start | bytes 9437184 | tf_op jit(solution)/shard_map/all_to_all | solution.py:17
  117.2 59.1 %all-to-all-done.6 = bf16[64,24,1536]{2,1,0:T(8,128)(2,1)} async-done(((bf16[64,24,1536]{2,1,0:T(8,128)(2,1)}), bf16[64,24,1536]{2,1,0:T(8,128)(2,1)}, u32[]{:S(2)}, u32[]{:S(2)}) %all-to-all-start.6) | async-done | bytes 4718624 | tf_op jit(solution)/shard_map/all_to_all | solution.py:17
  176.4 4.0 %convolution_convert_fusion = bf16[64,1536]{1,0:T(8,128)(2,1)} fusion(bf16[1536,64]{1,0:T(8,128)(2,1)S(1)} %bitcast.94, bf16[1536,1536]{1,0:T(8,128)(2,1)} %bitcast.20), kind=kOutput, calls=%fused_computation | convolution fusion | flops 302088192 | bytes 5111808 | tf_op jit(solution)/shard_map/dot_general | solution.py:126
  (35 shorter events, 8.8 us)
Async XLA Ops:
  0.0 13.1 %copy-start = (f32[24,16384]{1,0:T(8,128)S(1)}, f32[24,16384]{1,0:T(8,128)}, u32[]{:S(2)}) copy-start(f32[24,16384]{1,0:T(8,128)} %param.9) | copy-start | bytes 4718596
  1.8 21.8 %all-to-all-start.1 = ((bf16[4,6,4096]{2,1,0:T(8,128)(2,1)}), bf16[4,6,4096]{2,1,0:T(8,128)(2,1)}, u32[]{:S(2)}, u32[]{:S(2)}) async-start(bf16[4,6,4096]{2,1,0:T(8,128)(2,1)} %all_to_all.51), calls=%async_computation.1 | async-start | bytes 524288 | tf_op jit(solution)/shard_map/all_to_all | solution.py:103
  15.5 16.5 %copy-start.6 = (f32[24]{0:T(128)S(1)}, f32[24]{0:T(128)}, u32[]{:S(2)}) copy-start(f32[24]{0:T(128)} %param.10) | copy-start | bytes 292
  23.7 14.9 %all-to-all-start.2 = ((bf16[4,6,4096]{2,1,0:T(8,128)(2,1)}), bf16[4,6,4096]{2,1,0:T(8,128)(2,1)}, u32[]{:S(2)}, u32[]{:S(2)}) async-start(bf16[4,6,4096]{2,1,0:T(8,128)(2,1)} %all_to_all.53), calls=%async_computation.2 | async-start | bytes 524288 | tf_op jit(solution)/shard_map/all_to_all | solution.py:104
  38.6 27.0 %all-to-all-start = ((bf16[4,6,4096]{2,1,0:T(8,128)(2,1)}), bf16[4,6,4096]{2,1,0:T(8,128)(2,1)}, u32[]{:S(2)}, u32[]{:S(2)}) async-start(bf16[4,6,4096]{2,1,0:T(8,128)(2,1)} %all_to_all.49), calls=%async_computation | async-start | bytes 524288 | tf_op jit(solution)/shard_map/all_to_all | solution.py:102
  52.4 4.9 %copy-start.1 = (f32[6,256,128]{2,1,0:T(8,128)S(1)}, f32[6,256,128]{2,1,0:T(8,128)}, u32[]{:S(2)}) copy-start(f32[6,256,128]{2,1,0:T(8,128)} %fusion.39) | copy-start | bytes 2359300
  52.4 4.9 %copy-start.2 = (f32[6,256,128]{2,1,0:T(8,128)S(1)}, f32[6,256,128]{2,1,0:T(8,128)}, u32[]{:S(2)}) copy-start(f32[6,256,128]{2,1,0:T(8,128)} %convolution_add_fusion.2) | copy-start | bytes 2359300
  58.9 4.7 %copy-start.3 = (f32[256,256]{1,0:T(8,128)S(1)}, f32[256,256]{1,0:T(8,128)}, u32[]{:S(2)}) copy-start(f32[256,256]{1,0:T(8,128)} %fusion.36) | copy-start | bytes 786436
  60.1 4.4 %copy-start.4 = (f32[256,256]{1,0:T(8,128)S(1)}, f32[256,256]{1,0:T(8,128)}, u32[]{:S(2)}) copy-start(f32[256,256]{1,0:T(8,128)} %fusion.35) | copy-start | bytes 786436
  65.3 42.7 %copy-start.5 = (bf16[24,1536]{1,0:T(8,128)(2,1)S(1)}, bf16[24,1536]{1,0:T(8,128)(2,1)}, u32[]{:S(2)}) copy-start(bf16[24,1536]{1,0:T(8,128)(2,1)} %param.11) | copy-start | bytes 221188
  110.4 66.0 %all-to-all-start.6 = ((bf16[64,24,1536]{2,1,0:T(8,128)(2,1)}), bf16[64,24,1536]{2,1,0:T(8,128)(2,1)}, u32[]{:S(2)}, u32[]{:S(2)}) async-start(bf16[64,24,1536]{2,1,0:T(8,128)(2,1)} %stack.2), calls=%async_computation.6 | async-start | bytes 9437184 | tf_op jit(solution)/shard_map/all_to_all | solution.py:17
